TPU v7x, 256 devices: a 4x2x16 block of a 4x16x16 slice. The times are simulated.
256 devices in a mesh: rep: 2 (over y), tp: 32 (over z, core), sub: 4 (over x).
Axes of the slice: x: 4, y: 2, z: 16, core: 2. Of those that a mesh axis runs over, the one named last changes fastest.
The devices are a block of a 4x16x16 slice.
Arguments:
- hidden_in: bfloat16 [128, 6144], P(('rep', 'sub'), 'tp'), parts along dimension 0, may hold values from -128 to 128
- query: bfloat16 [128, 6144], P(('rep', 'sub'), 'tp'), parts along dimension 0, may hold values from -128 to 128
- key_new: bfloat16 [128, 1024], P(('rep', 'sub'), 'tp'), parts along dimension 0, may hold values from -8 to 8
- value_new: bfloat16 [128, 1024], P(('rep', 'sub'), 'tp'), parts along dimension 0, may hold values from -6 to 6
- key_cache: bfloat16 [128, 1024, 1024], P(('rep', 'sub'), 'tp'), parts along dimension 0, may hold values from -8 to 8
- value_cache: bfloat16 [128, 1024, 1024], P(('rep', 'sub'), 'tp'), parts along dimension 0, may hold values from -6 to 6
- lengths: int32 [128], P(('rep', 'sub')), parts along dimension 0, may hold values from 2 to 1024
- out_weight: bfloat16 [6144, 6144], P('sub', 'tp'), may hold values from -0.078125 to 0.078125
- norm_gain: bfloat16 [6144], P('tp'), may hold values from 0.099609375 to 1.8984375
- router_weight: bfloat16 [6144, 4], P('tp'), may hold values from -0.078125 to 0.078125
- routes: int32 [128, 2], P(('rep', 'sub')), parts along dimension 0, may hold values from 0 to 3, all different within a row; in each aligned block of 16 rows (0 to 15, 16 to 31, ...) at most 12 rows name the same one
- gate_weight: bfloat16 [4, 6144, 8192], P('sub', None, 'tp'), may hold values from -0.078125 to 0.078125
- up_weight: bfloat16 [4, 6144, 8192], P('sub', None, 'tp'), may hold values from -0.078125 to 0.078125
- down_weight: bfloat16 [4, 8192, 6144], P('sub', 'tp'), may hold values from -0.125 to 0.125
Outputs:
- layer_out: bfloat16 [128, 6144], P(('rep', 'sub'), 'tp'), parts along dimension 0
There are 2 independent parts, one for each index of `rep`. A program takes and returns all parts, laid end to end along the dimension named above; an argument that names none is the same for every part. Nothing has to cross between parts.
Inputs may be any that keep to these rules, and one draw needn't show every extreme that they name: `routes`: the two experts of a row differ; within the 16 rows of one index of sub, no expert is named by more than 12 rows, a bound that some such block reaches.
All inputs are finite; a program needn't handle non-finite values.
Results may differ from a plain program's by a relative error of at most 0.0075.
Values may be sent and summed in bfloat16 or wider, within the bound.
A program may use at most 128 MiB of HBM per device.

v0:
```python
import jax
import jax.numpy as jnp
from jax import lax
from jax.sharding import Mesh
from jax.sharding import PartitionSpec as P

D = 6144
H = 48
KVH = 8
HD = 128
E = 4
MOST = 12
TP = ("tp_0", "tp_1")


def side_by_side(arrays, axis, dim, along):
    ends, at = ([], 0)
    for a in arrays[:-1]:
        at += a.shape[along]
        ends.append(at)
    both = jnp.concatenate(arrays, axis=along)
    return tuple(jnp.split(lax.all_gather(both, axis, axis=dim, tiled=True), ends, axis=along))


def combined_by_axis(value, axes, combine):
    for axis in axes:
        pieces = jax.tree.map(lambda part: lax.all_gather(part, axis), value)
        value = jax.tree.map(lambda part: part[0], pieces)
        for k in range(1, lax.axis_size(axis)):
            value = combine(value, jax.tree.map(lambda part: part[k], pieces))
    return value


def in_order(parts, dim):
    parts = jnp.moveaxis(parts, 0, dim)
    dims = parts.shape
    return parts.reshape(*dims[:dim], dims[dim] * dims[dim + 1], *dims[dim + 2 :])


def sent_to_all(value, axis):
    count = lax.axis_size(axis)
    return lax.all_to_all(
        jnp.broadcast_to(value[None], (count, *value.shape)), axis, 0, 0, tiled=True
    )


def gathered_copies(value, axis, dim):
    return in_order(sent_to_all(value, axis), dim)


def taken_together(value, axis):
    return sent_to_all(value, axis).sum(axis=0)


def all_blocks(value, axes, order):
    parts = value
    for k in order:
        parts = lax.all_gather(parts, axes[k])
    done = order[::-1]
    back = [done.index(k) for k in range(len(axes))]
    parts = parts.transpose(*back, *range(len(axes), parts.ndim))
    return parts.reshape(-1, *value.shape)


def gather_axes(value, axes, order, dim):
    return in_order(all_blocks(value, axes, order), dim)


def in_blocks(value, dim, count):
    dims = value.shape
    parts = value.reshape(*dims[:dim], count, dims[dim] // count, *dims[dim + 1 :])
    return jnp.moveaxis(parts, dim, 0)


def summed_on_arrival(value, axis, dim):
    count = lax.axis_size(axis)
    parts = lax.all_to_all(in_blocks(value, dim, count), axis, 0, 0, tiled=True)
    return jnp.sum(parts, axis=0)


def join_softmax(first, second):
    joined = jnp.maximum(first[0], second[0])
    first_scale = jnp.exp(first[0] - joined)
    second_scale = jnp.exp(second[0] - joined)
    totals = first[1] * first_scale + second[1] * second_scale
    summed = first[2] * first_scale[..., None] + second[2] * second_scale[..., None]
    return (joined, totals, summed)


def on_device(
    hidden_in,
    query,
    key_new,
    value_new,
    key_cache,
    value_cache,
    lengths,
    out_weight,
    norm_gain,
    router_weight,
    routes,
    gate_weight,
    up_weight,
    down_weight,
):
    seq_rows = hidden_in.shape[0]
    group_size = H // KVH
    scale_factor = 1.0 / HD**0.5
    local_len = key_cache.shape[1]
    all_query, all_key, all_value = (
        lax.all_gather(query, TP, axis=1, tiled=True),
        *side_by_side((key_new, value_new), TP, 1, 0),
    )
    query_rows = all_query.reshape(seq_rows, KVH, group_size, HD)
    cached_keys = key_cache.reshape(seq_rows, local_len, KVH, HD)
    cached_values = value_cache.reshape(seq_rows, local_len, KVH, HD).astype(jnp.float32)
    scores = (
        jnp.einsum("bkgd,bpkd->bkgp", query_rows, cached_keys, preferred_element_type=jnp.float32)
        * scale_factor
    )
    positions = lax.axis_index(TP) * local_len + jnp.arange(local_len, dtype=jnp.int32)
    valid = positions[None, :] < lengths[:, None]
    scores = jnp.where(valid[:, None, None, :], scores, -jnp.inf)
    owned_part = (
        jnp.einsum(
            "zyqn,zyn->zyq",
            query_rows,
            all_key.reshape(seq_rows, KVH, HD),
            preferred_element_type=jnp.float32,
        )
        * scale_factor
    )
    local_max = jnp.maximum(jnp.max(scores, axis=-1), owned_part)
    weights = jnp.exp(scores - local_max[..., None])
    partial_total = jnp.sum(weights, axis=-1)
    local_summed = jnp.einsum("bkgp,bpkd->bkgd", weights, cached_values)
    run_max, total, summed = combined_by_axis(
        (local_max, partial_total, local_summed), TP, join_softmax
    )
    own_weight = jnp.exp(owned_part - run_max)
    total = total + own_weight
    new_values = all_value.reshape(seq_rows, KVH, 1, HD).astype(jnp.float32)
    summed = summed + own_weight[..., None] * new_values
    attn = (summed / total[..., None]).reshape(seq_rows, H * HD).astype(jnp.bfloat16)
    column_span = attn
    projected = jnp.dot(
        column_span, gathered_copies(out_weight, "sub", 0), preferred_element_type=jnp.float32
    )
    resid = hidden_in.astype(jnp.float32) + projected
    gain_full = norm_gain.astype(jnp.float32)[None, :]
    router_full = router_weight.astype(jnp.float32)
    squares = taken_together(jnp.sum(resid * resid, axis=-1), TP)
    root = jnp.sqrt(squares / D + 1e-05)
    normed = resid / root[:, None] * gain_full
    logits = taken_together(jnp.dot(normed, router_full), TP)
    normed_low = normed.astype(jnp.bfloat16)
    expert_ids = jnp.arange(E, dtype=jnp.int32)[None, :]
    first_hot = (routes[:, 0:1] == expert_ids).astype(jnp.float32)
    second_hot = (routes[:, 1:2] == expert_ids).astype(jnp.float32)
    first_logit = jnp.sum(logits * first_hot, axis=-1)
    second_logit = jnp.sum(logits * second_hot, axis=-1)
    first_weight = 1.0 / (1.0 + jnp.exp(second_logit - first_logit))
    second_weight = 1.0 / (1.0 + jnp.exp(first_logit - second_logit))
    dense = first_weight[:, None] * first_hot + second_weight[:, None] * second_hot
    gate_local = gate_weight[0]
    up_local = up_weight[0]
    down_local = down_weight[0]
    routed_mask = first_hot + second_hot
    rank = jnp.cumsum(routed_mask, axis=0) - routed_mask
    slot_ids = jnp.arange(MOST, dtype=jnp.float32)
    selector = routed_mask.T[:, None, :] * (rank.T[:, None, :] == slot_ids[None, :, None]).astype(
        jnp.float32
    )
    send_rows = jnp.einsum(
        "emb,bc->emc", selector.astype(jnp.bfloat16), normed_low, preferred_element_type=jnp.float32
    ).astype(jnp.bfloat16)
    received = lax.all_to_all(send_rows, "sub", split_axis=0, concat_axis=0, tiled=True)
    sources, slots, column_span = received.shape
    piece = gather_axes(received.reshape(sources * slots, column_span), TP, (0, 1), 1)
    gate_out = jnp.dot(piece, gate_local, preferred_element_type=jnp.float32)
    up_out = jnp.dot(piece, up_local, preferred_element_type=jnp.float32)
    inner = (jax.nn.silu(gate_out) * up_out).astype(jnp.bfloat16)
    result = jnp.dot(inner, down_local, preferred_element_type=jnp.float32)
    outputs = summed_on_arrival(result, TP, 1).reshape(sources, slots, column_span)
    returned = lax.all_to_all(outputs, "sub", split_axis=0, concat_axis=0, tiled=True)
    weighted = selector * dense.T[:, None, :]
    mixed = jnp.einsum("emb,emc->bc", weighted, returned)
    return (resid + mixed).astype(jnp.bfloat16)


def solution(mesh):
    split = Mesh(
        mesh.devices.reshape(mesh.shape["rep"], 16, 2, mesh.shape["sub"]),
        ("rep", "tp_0", "tp_1", "sub"),
    )
    return jax.shard_map(
        on_device,
        mesh=split,
        in_specs=(
            P(("rep", "sub"), TP),
            P(("rep", "sub"), TP),
            P(("rep", "sub"), TP),
            P(("rep", "sub"), TP),
            P(("rep", "sub"), TP, None),
            P(("rep", "sub"), TP, None),
            P(("rep", "sub")),
            P("sub", TP),
            P(TP),
            P(TP, None),
            P(("rep", "sub"), None),
            P("sub", None, TP),
            P("sub", None, TP),
            P("sub", TP, None),
        ),
        out_specs=P(("rep", "sub"), TP),
        check_vma=False,
    )
```

profile of v0, /device:TPU:40, one launch (start us, length us, event | category | flops | bytes accessed | tf_op | source)
XLA Modules:
  0.0 523.5 jit_solution(8818489390149967905)
XLA Ops:
  6.6 50.3 %all-gather.4 = bf16[32,192,16]{1,2,0:T(8,128)(2,1)S(1)} all-gather(bf16[1,192,16]{1,2,0:T(8,128)(2,1)} %bitcast.708), channel_id=1, replica_groups=mesh['rep'=2,'tp_0'=16,'tp_1'=2,'sub'=4] {'tp_0','tp_1'}, dimensions={0}, use_global_device_ids=true | all-gather | bytes 202752 | tf_op jit(solution)/shard_map/all_gather | solution.py:111
  57.9 1.9 reshape.1214
  61.4 27.9 %all_gather.46 = bf16[32,1024]{0,1:T(8,128)(2,1)S(1)} all-gather(bf16[32,32]{0,1:T(8,128)(2,1)S(1)} %pad_maximum_fusion), channel_id=1, replica_groups=mesh['rep'=2,'tp_0'=16,'tp_1'=2,'sub'=4] {'tp_0','tp_1'}, dimensions={1}, use_global_device_ids=true | all-gather | bytes 67584 | tf_op jit(solution)/shard_map/all_gather | solution.py:22
  92.5 2.1 fusion.172
  95.4 1.7 fusion.16
  97.9 2.7 broadcast_in_dim.20
  100.7 4.6 all-to-all-start
  105.3 45.4 %all-gather.1 = f32[256,8,6]{2,1,0:T(8,128)S(1)} all-gather(f32[16,8,6]{2,1,0:T(8,128)S(1)} %multiply_maximum_fusion), channel_id=3, replica_groups=mesh['rep'=2,'tp_0'=16,'tp_1'=2,'sub'=4] {'tp_0'}, dimensions={0}, use_global_device_ids=true | all-gather | bytes 52224 | tf_op jit(solution)/shard_map/all_gather | solution.py:27
  151.7 1.6 copy.411
  153.3 1.6 copy.413
  154.8 1.6 copy.415
  160.0 1.6 copy.410
  164.7 1.6 copy.416
  171.0 1.6 copy.424
  172.5 1.6 copy.425
  175.0 1.9 all_gather.52
  182.0 32.6 %all-gather.2 = f32[256,8,6]{2,1,0:T(8,128)S(1)} all-gather(f32[16,8,6]{2,1,0:T(8,128)S(1)} %fusion.23), channel_id=4, replica_groups=mesh['rep'=2,'tp_0'=16,'tp_1'=2,'sub'=4] {'tp_0'}, dimensions={0}, use_global_device_ids=true | all-gather | bytes 52224 | tf_op jit(solution)/shard_map/all_gather | solution.py:27
  217.1 1.6 copy.429
  218.7 1.6 copy.430
  220.3 1.6 copy.431
  223.4 1.6 copy.433
  225.0 1.6 copy.434
  228.1 1.6 copy.436
  235.9 1.6 copy.441
  239.0 1.6 copy.443
  241.8 1.9 all_gather.55
  247.3 1.7 fusion.77
  249.0 1.6 copy.372
  250.6 1.6 copy.373
  252.2 1.6 copy.374
  253.9 1.6 copy.394
  309.0 3.5 copy.448
  312.5 7.3 %fusion.30 = f32[1,16,8,6,128]{4,2,3,1,0:T(8,128)S(1)} fusion(f32[256,8,6,128]{3,1,2,0:T(8,128)} %all-gather.7.cloned.1.call-done, f32[16,8,6]{1,2,0:T(8,128)S(1)} %copy-done.6, f32[16,8,6]{1,2,0:T(8,128)S(1)} %copy-done.5, f32[16,8,6]{1,2,0:T(8,128)S(1)} %copy-done.4, f32[16,8,6]{1,2,0:T(8,128)S(1)} %copy.365, f32[16,8,6]{1,2,0:T(8,128)S(1)} %copy.363, ...), kind=kLoop, calls=%fused_computation.31 | loop fusion | flops 4423680 | bytes 6776832 | tf_op jit(solution)/shard_map/add | solution.py:86
  319.9 2.6 all_gather.51
  324.0 2.6 multiply_reduce_fusion
  327.2 7.8 %all-to-all-start.1 = ((f32[32,1,16]{2,1,0:T(1,128)}), f32[32,1,16]{2,1,0:T(1,128)S(1)}, u32[]{:S(2)}, u32[]{:S(2)}) async-start(f32[32,1,16]{2,1,0:T(1,128)} %broadcast_in_dim.21), calls=%async_computation.1 | async-start | bytes 32768 | tf_op jit(solution)/shard_map/all_to_all | solution.py:42
  335.0 11.8 %all-to-all-done.1 = f32[32,1,16]{2,1,0:T(1,128)S(1)} async-done(((f32[32,1,16]{2,1,0:T(1,128)}), f32[32,1,16]{2,1,0:T(1,128)S(1)}, u32[]{:S(2)}, u32[]{:S(2)}) %all-to-all-start.1) | async-done | bytes 2080 | tf_op jit(solution)/shard_map/all_to_all | solution.py:42
  347.7 4.7 all-to-all-start.2
  352.5 13.6 %all-to-all-done.2 = f32[32,16,4]{1,2,0:T(4,128)S(1)} async-done(((f32[32,16,4]{1,2,0:T(4,128)}), f32[32,16,4]{1,2,0:T(4,128)S(1)}, u32[]{:S(2)}, u32[]{:S(2)}) %all-to-all-start.2) | async-done | bytes 8224 | tf_op jit(solution)/shard_map/all_to_all | solution.py:42
  367.4 4.9 all-to-all-start.3
  372.3 4.7 copy.405
  377.8 28.9 %all_gather.56 = bf16[16,48,192]{2,1,0:T(8,128)(2,1)S(1)} all-gather(bf16[1,48,192]{2,1,0:T(8,128)(2,1)S(1)} %all_gather_reshape.3), channel_id=1, replica_groups=mesh['rep'=2,'tp_0'=16,'tp_1'=2,'sub'=4] {'tp_0'}, dimensions={0}, use_global_device_ids=true | all-gather | bytes 313344 | tf_op jit(solution)/shard_map/all_gather | solution.py:58
  406.6 2.4 all-gather.3
  410.2 2.6 reshape.1220
  412.8 2.7 fusion.2
  415.6 5.6 %convolution_bitcast_fusion = f32[32,48,192]{2,1,0:T(8,128)} fusion(bf16[32,192,256]{2,1,0:T(8,128)(2,1)} %bitcast.699, bf16[48,6144]{1,0:T(8,128)(2,1)} %reshape.1220, bf16[1,6144,256]{2,1,0:T(8,128)(2,1)S(1)} %copy-done, f32[48,256]{1,0:T(8,128)S(1)} %fusion.2), kind=kOutput, calls=%fused_computation.4 | convolution fusion | flops 302063616 | bytes 8110080 | tf_op jit(solution)/shard_map/dot_general | solution.py:183
  421.1 83.8 %all_to_all.31 = f32[32,48,192]{2,1,0:T(8,128)} all-to-all(f32[32,48,192]{2,1,0:T(8,128)} %convolution_bitcast_fusion), channel_id=1, replica_groups=mesh['rep'=2,'tp_0'=16,'tp_1'=2,'sub'=4] {'tp_0','tp_1'}, dimensions={0} | all-to-all | bytes 2359296 | tf_op jit(solution)/shard_map/all_to_all | solution.py:77
  506.4 9.4 %all_to_all.32 = bf16[4,12,192]{2,1,0:T(8,128)(2,1)S(1)} all-to-all(bf16[4,12,192]{2,1,0:T(8,128)(2,1)S(1)} %reshape.1221), channel_id=1, replica_groups=mesh['rep'=2,'tp_0'=16,'tp_1'=2,'sub'=4] {'sub'}, dimensions={0} | all-to-all | bytes 36864 | tf_op jit(solution)/shard_map/all_to_all | solution.py:185
  (149 shorter events, 106.4 us)
Async XLA Ops:
  6.5 409.0 %copy-start = (bf16[1,6144,256]{2,1,0:T(8,128)(2,1)S(1)}, bf16[1,6144,256]{2,1,0:T(8,128)(2,1)}, u32[]{:S(2)}) copy-start(bf16[1,6144,256]{2,1,0:T(8,128)(2,1)} %param.26) | copy-start | bytes 9437188
  6.6 84.6 %copy-start.16 = (s32[16]{0:T(128)S(1)}, s32[16]{0:T(128)}, u32[]{:S(2)}) copy-start(s32[16]{0:T(128)} %param.20) | copy-start | bytes 196
  6.6 305.9 %all-gather.7.cloned.1.call-start = ((), (), s32[]{:S(2)}) async-start(), calls=%async_computation.6 | async-start | bytes 6684672 | tf_op jit(solution)/shard_map/all_gather | solution.py:27
  92.5 2.1 copy-start.8
  94.6 0.8 copy-start.1
  100.7 208.3 %all-to-all-start = ((bf16[4,1536,192]{1,2,0:T(8,128)(2,1)}), bf16[4,1536,192]{1,2,0:T(8,128)(2,1)}, u32[]{:S(2)}, u32[]{:S(2)}) async-start(bf16[4,1536,192]{1,2,0:T(8,128)(2,1)} %broadcast_in_dim.20), calls=%async_computation | async-start | bytes 4718592 | tf_op jit(solution)/shard_map/all_to_all | solution.py:42
  182.0 58.6 %copy-start.2 = (f32[16,8,6]{0,1,2:T(8,128)S(1)}, f32[16,8,6]{0,1,2:T(8,128)}, u32[]{:S(2)}) copy-start(f32[16,8,6]{0,1,2:T(8,128)} %copy.417) | copy-start | bytes 9220
  182.0 58.6 %copy-start.3 = (f32[16,8,6]{0,1,2:T(8,128)S(1)}, f32[16,8,6]{0,1,2:T(8,128)}, u32[]{:S(2)}) copy-start(f32[16,8,6]{0,1,2:T(8,128)} %copy.415) | copy-start | bytes 9220
  308.9 3.5 copy-start.4
  308.9 3.5 copy-start.5
  309.0 3.5 copy-start.6
  309.0 3.5 copy-start.7
  312.5 10.0 %copy-start.9 = (f32[16,8,128]{2,1,0:T(8,128)S(1)}, f32[16,8,128]{2,1,0:T(8,128)}, u32[]{:S(2)}) copy-start(f32[16,8,128]{2,1,0:T(8,128)} %copy.375) | copy-start | bytes 196612
  312.5 10.0 %copy-start.10 = (f32[16,8,6]{1,2,0:T(8,128)S(1)}, f32[16,8,6]{1,2,0:T(8,128)}, u32[]{:S(2)}) copy-start(f32[16,8,6]{1,2,0:T(8,128)} %copy.372) | copy-start | bytes 9220
  312.5 10.0 %copy-start.11 = (f32[16,8,6]{1,2,0:T(8,128)S(1)}, f32[16,8,6]{1,2,0:T(8,128)}, u32[]{:S(2)}) copy-start(f32[16,8,6]{1,2,0:T(8,128)} %copy.373) | copy-start | bytes 9220
  312.5 10.0 %copy-start.12 = (f32[16,8,6]{1,2,0:T(8,128)S(1)}, f32[16,8,6]{1,2,0:T(8,128)}, u32[]{:S(2)}) copy-start(f32[16,8,6]{1,2,0:T(8,128)} %copy.374) | copy-start | bytes 9220
  312.5 10.0 %copy-start.13 = (f32[16,8,6]{1,2,0:T(8,128)S(1)}, f32[16,8,6]{1,2,0:T(8,128)}, u32[]{:S(2)}) copy-start(f32[16,8,6]{1,2,0:T(8,128)} %copy.394) | copy-start | bytes 9220
  319.8 4.1 copy-start.14
  319.9 15.2 %copy-start.18 = (bf16[192]{0:T(256)(128)(2,1)S(1)}, bf16[192]{0:T(256)(128)(2,1)}, u32[]{:S(2)}) copy-start(bf16[192]{0:T(256)(128)(2,1)} %param.22) | copy-start | bytes 1156
  319.9 27.0 %copy-start.17 = (bf16[192,4]{0,1:T(4,128)(2,1)S(1)}, bf16[192,4]{0,1:T(4,128)(2,1)}, u32[]{:S(2)}) copy-start(bf16[192,4]{0,1:T(4,128)(2,1)} %param.23) | copy-start | bytes 4612
  319.9 32.6 %copy-start.15 = (s32[16,2]{0,1:T(2,128)S(1)}, s32[16,2]{0,1:T(2,128)}, u32[]{:S(2)}) copy-start(s32[16,2]{0,1:T(2,128)} %param.24) | copy-start | bytes 388
  327.2 19.6 %all-to-all-start.1 = ((f32[32,1,16]{2,1,0:T(1,128)}), f32[32,1,16]{2,1,0:T(1,128)S(1)}, u32[]{:S(2)}, u32[]{:S(2)}) async-start(f32[32,1,16]{2,1,0:T(1,128)} %broadcast_in_dim.21), calls=%async_computation.1 | async-start | bytes 32768 | tf_op jit(solution)/shard_map/all_to_all | solution.py:42
  347.7 18.3 %all-to-all-start.2 = ((f32[32,16,4]{1,2,0:T(4,128)}), f32[32,16,4]{1,2,0:T(4,128)S(1)}, u32[]{:S(2)}, u32[]{:S(2)}) async-start(f32[32,16,4]{1,2,0:T(4,128)} %broadcast_in_dim.22), calls=%async_computation.2 | async-start | bytes 131072 | tf_op jit(solution)/shard_map/all_to_all | solution.py:42
  367.4 10.3 %all-to-all-start.3 = ((bf16[4,12,192]{2,1,0:T(8,128)(2,1)}), bf16[4,12,192]{2,1,0:T(8,128)(2,1)S(1)}, u32[]{:S(2)}, u32[]{:S(2)}) async-start(bf16[4,12,192]{2,1,0:T(8,128)(2,1)} %convolution_convert_fusion), calls=%async_computation.3 | async-start | bytes 65536 | tf_op jit(solution)/shard_map/all_to_all | solution.py:177
Sparse Core Ops, SparseCore 0:
  98.1 87.2 all-gather.6
where the time goes:
time: 529 us; the launch traced here: 523 us
  blocking collectives  287 us (54%)
  local copies, waits for them, and re-layouts  131 us (25%)
  other arithmetic  26.3 us (5%)
  waiting for transfers between devices  26.2 us (5%)
  starting transfers between devices  22 us (4%)
  matrix products  17.6 us (3%)
  between operations  13.8 us (3%)
    all_gather x5, blocking collectives, combined_by_axis(): pieces = jax.tree.map(lambda part: lax.all_gather(part, axis), value)  84.3 us
    all_to_all x1, blocking collectives, summed_on_arrival(): parts = lax.all_to_all(in_blocks(value, dim, count), axis, 0, 0, tiled=True)  83.8 us
    unnamed x78, local copies, waits for them, and re-layouts  61.3 us
    all_gather x1, blocking collectives, on_device(): lax.all_gather(query, TP, axis=1, tiled=True)  50.3 us
    all_gather x2, blocking collectives, all_blocks(): parts = lax.all_gather(parts, axes[k])  31.2 us
    all_gather x1, blocking collectives, side_by_side(): lax.all_gather(both, axis, axis=dim, tiled=True)  27.9 us
    all_to_all x3, waiting for transfers between devices, sent_to_all(): lax.all_to_all(jnp.broadcast_to(value[None], (count, *value.shape)), axis...  25.3 us
    exp x16, local copies, waits for them, and re-layouts, join_softmax(): first_scale = jnp.exp(first[0] - joined)  22.7 us
  transfers between devices with their start and end apart: 5, of which 3 were waited for; matrix products, arithmetic and copies ran while one was open for 25% of the time, Pallas kernels for 0%

commit v1 on v0

--- a/solution.py
+++ b/solution.py
@@ -108,7 +108,7 @@
     scale_factor = 1.0 / HD**0.5
     local_len = key_cache.shape[1]
     all_query, all_key, all_value = (
-        lax.all_gather(query, TP, axis=1, tiled=True),
+        jnp.concatenate(lax.all_to_all(jnp.stack([query] * lax.axis_size(TP)), TP, 0, 0), axis=1),
         *side_by_side((key_new, value_new), TP, 1, 0),
     )
     query_rows = all_query.reshape(seq_rows, KVH, group_size, HD)

time: 529 us -> 499 us (0.943)
  blocking collectives: 287 us -> 251 us
  starting transfers between devices: 22 us -> 49.5 us
  local copies, waits for them, and re-layouts: 131 us -> 117 us
  other arithmetic: 26.3 us -> 20.1 us
    all_gather x1 -> x0, blocking collectives: 50.3 us -> none  [on_device(): lax.all_gather(query, TP, axis=1, tiled=True)]
    all_to_all x0 -> x1, starting transfers between devices: none -> 24.7 us  [on_device(): lax.all_to_all(jnp.stack([query] * lax.axis_size(TP)), TP, 0, 0)]
    unnamed x78 -> x69, local copies, waits for them, and re-layouts: 61.3 us -> 51.3 us
    all_gather x1, blocking collectives: 27.9 us -> 36.8 us  [side_by_side(): lax.all_gather(both, axis, axis=dim, tiled=True)]
    exp x8, other arithmetic: 11.3 us -> 4.65 us  [join_softmax(): first_scale = jnp.exp(first[0] - joined)]
  transfers between devices with their start and end apart: 5 -> 6, of which waited for: 3 -> 3; matrix products, arithmetic and copies ran while one was open for 25% -> 23% of each run, Pallas kernels for 0% -> 0%
where the time goes in v1:
time: 499 us; the launch traced here: 494 us
  blocking collectives  251 us (50%)
  local copies, waits for them, and re-layouts  117 us (23%)
  starting transfers between devices  49.5 us (10%)
  waiting for transfers between devices  26.2 us (5%)
  other arithmetic  20.1 us (4%)
  matrix products  16.6 us (3%)
  between operations  13.8 us (3%)
    all_gather x5, blocking collectives, combined_by_axis(): pieces = jax.tree.map(lambda part: lax.all_gather(part, axis), value)  89.5 us
    all_to_all x1, blocking collectives, summed_on_arrival(): parts = lax.all_to_all(in_blocks(value, dim, count), axis, 0, 0, tiled=True)  83.8 us
    unnamed x69, local copies, waits for them, and re-layouts  51.3 us
    all_gather x1, blocking collectives, side_by_side(): lax.all_gather(both, axis, axis=dim, tiled=True)  36.8 us
    all_gather x2, blocking collectives, all_blocks(): parts = lax.all_gather(parts, axes[k])  31.3 us
    all_to_all x3, waiting for transfers between devices, sent_to_all(): lax.all_to_all(jnp.broadcast_to(value[None], (count, *value.shape)), axis...  25.3 us
    all_to_all x1, starting transfers between devices, on_device(): lax.all_to_all(jnp.stack([query] * lax.axis_size(TP)), TP, 0, 0)  24.7 us
    exp x16, local copies, waits for them, and re-layouts, join_softmax(): first_scale = jnp.exp(first[0] - joined)  20.6 us
  transfers between devices with their start and end apart: 6, of which 3 were waited for; matrix products, arithmetic and copies ran while one was open for 23% of the time, Pallas kernels for 0%

profile of v1, /device:TPU:40, one launch (start us, length us, event | category | flops | bytes accessed | tf_op | source)
XLA Modules:
  0.0 493.8 jit_solution(3439003489643038062)
XLA Ops:
  6.6 1.6 stack.2
  8.1 24.7 %all-to-all-start = ((bf16[32,16,192]{2,1,0:T(8,128)(2,1)}), bf16[32,16,192]{2,1,0:T(8,128)(2,1)S(1)}, u32[]{:S(2)}, u32[]{:S(2)}) async-start(bf16[32,16,192]{2,1,0:T(8,128)(2,1)} %stack.2), calls=%async_computation | async-start | bytes 524288 | tf_op jit(solution)/shard_map/all_to_all | solution.py:111
  34.6 36.8 %all_gather.42 = bf16[32,1024]{0,1:T(8,128)(2,1)S(1)} all-gather(bf16[32,32]{0,1:T(8,128)(2,1)S(1)} %pad_maximum_fusion), channel_id=1, replica_groups=mesh['rep'=2,'tp_0'=16,'tp_1'=2,'sub'=4] {'tp_0','tp_1'}, dimensions={1}, use_global_device_ids=true | all-gather | bytes 67584 | tf_op jit(solution)/shard_map/all_gather | solution.py:22
  76.5 2.0 fusion.172
  79.3 1.7 fusion.16
  81.9 2.8 broadcast_in_dim.20
  84.6 4.6 all-to-all-start.1
  90.0 42.5 %all-gather.1 = f32[256,8,6]{2,1,0:T(8,128)S(1)} all-gather(f32[16,8,6]{2,1,0:T(8,128)S(1)} %multiply_maximum_fusion), channel_id=3, replica_groups=mesh['rep'=2,'tp_0'=16,'tp_1'=2,'sub'=4] {'tp_0'}, dimensions={0}, use_global_device_ids=true | all-gather | bytes 52224 | tf_op jit(solution)/shard_map/all_gather | solution.py:27
  138.5 1.6 copy.409
  147.5 1.9 all_gather.48
  154.5 40.8 %all-gather.2 = f32[256,8,6]{2,1,0:T(8,128)S(1)} all-gather(f32[16,8,6]{2,1,0:T(8,128)S(1)} %fusion.23), channel_id=4, replica_groups=mesh['rep'=2,'tp_0'=16,'tp_1'=2,'sub'=4] {'tp_0'}, dimensions={0}, use_global_device_ids=true | all-gather | bytes 52224 | tf_op jit(solution)/shard_map/all_gather | solution.py:27
  196.4 1.6 copy.427
  197.9 1.6 copy.428
  199.5 1.6 copy.429
  201.1 1.6 copy.430
  202.6 1.6 copy.431
  204.2 1.6 copy.432
  205.8 1.6 copy.433
  207.3 1.6 copy.434
  208.9 1.6 copy.435
  212.0 1.6 copy.437
  213.6 1.6 copy.438
  215.1 1.6 copy.439
  216.7 1.6 copy.440
  219.8 1.6 copy.442
  222.5 1.9 all_gather.51
  228.0 1.7 fusion.77
  229.7 1.6 copy.371
  231.3 1.6 copy.372
  232.9 1.6 copy.373
  234.6 1.6 copy.393
  276.9 3.4 copy.447
  280.4 7.3 %fusion.30 = f32[1,16,8,6,128]{4,2,3,1,0:T(8,128)S(1)} fusion(f32[256,8,6,128]{3,1,2,0:T(8,128)} %all-gather.6.cloned.1.call-done, f32[16,8,6]{1,2,0:T(8,128)S(1)} %copy.368, f32[16,8,6]{1,2,0:T(8,128)S(1)} %copy.367, f32[16,8,6]{1,2,0:T(8,128)S(1)} %copy.365, f32[16,8,6]{1,2,0:T(8,128)S(1)} %copy.364, f32[16,8,6]{1,2,0:T(8,128)S(1)} %copy.362, ...), kind=kLoop, calls=%fused_computation.31 | loop fusion | flops 4423680 | bytes 6776832 | tf_op jit(solution)/shard_map/add | solution.py:86
  287.8 2.4 all_gather.47
  291.7 2.6 multiply_reduce_fusion
  294.9 10.2 %all-to-all-start.2 = ((f32[32,1,16]{2,1,0:T(1,128)}), f32[32,1,16]{2,1,0:T(1,128)S(1)}, u32[]{:S(2)}, u32[]{:S(2)}) async-start(f32[32,1,16]{2,1,0:T(1,128)} %broadcast_in_dim.21), calls=%async_computation.2 | async-start | bytes 32768 | tf_op jit(solution)/shard_map/all_to_all | solution.py:42
  305.2 11.8 %all-to-all-done.2 = f32[32,1,16]{2,1,0:T(1,128)S(1)} async-done(((f32[32,1,16]{2,1,0:T(1,128)}), f32[32,1,16]{2,1,0:T(1,128)S(1)}, u32[]{:S(2)}, u32[]{:S(2)}) %all-to-all-start.2) | async-done | bytes 2080 | tf_op jit(solution)/shard_map/all_to_all | solution.py:42
  317.8 4.8 all-to-all-start.3
  322.6 13.6 %all-to-all-done.3 = f32[32,16,4]{1,2,0:T(4,128)S(1)} async-done(((f32[32,16,4]{1,2,0:T(4,128)}), f32[32,16,4]{1,2,0:T(4,128)S(1)}, u32[]{:S(2)}, u32[]{:S(2)}) %all-to-all-start.3) | async-done | bytes 8224 | tf_op jit(solution)/shard_map/all_to_all | solution.py:42
  337.5 5.1 %all-to-all-start.4 = ((bf16[4,12,192]{2,1,0:T(8,128)(2,1)}), bf16[4,12,192]{2,1,0:T(8,128)(2,1)S(1)}, u32[]{:S(2)}, u32[]{:S(2)}) async-start(bf16[4,12,192]{2,1,0:T(8,128)(2,1)} %convolution_convert_fusion), calls=%async_computation.4 | async-start | bytes 65536 | tf_op jit(solution)/shard_map/all_to_all | solution.py:177
  342.6 4.7 copy.404
  348.1 28.9 %all_gather.52 = bf16[16,48,192]{2,1,0:T(8,128)(2,1)S(1)} all-gather(bf16[1,48,192]{2,1,0:T(8,128)(2,1)S(1)} %all_gather_reshape.3), channel_id=1, replica_groups=mesh['rep'=2,'tp_0'=16,'tp_1'=2,'sub'=4] {'tp_0'}, dimensions={0}, use_global_device_ids=true | all-gather | bytes 313344 | tf_op jit(solution)/shard_map/all_gather | solution.py:58
  377.0 2.4 all-gather.3
  380.6 2.6 reshape.1222
  383.2 2.7 fusion.2
  385.9 5.6 %convolution_bitcast_fusion = f32[32,48,192]{2,1,0:T(8,128)} fusion(bf16[32,192,256]{2,1,0:T(8,128)(2,1)} %bitcast.694, bf16[48,6144]{1,0:T(8,128)(2,1)} %reshape.1222, bf16[1,6144,256]{2,1,0:T(8,128)(2,1)S(1)} %copy-done, f32[48,256]{1,0:T(8,128)S(1)} %fusion.2), kind=kOutput, calls=%fused_computation.4 | convolution fusion | flops 302063616 | bytes 8110080 | tf_op jit(solution)/shard_map/dot_general | solution.py:183
  391.5 83.8 %all_to_all.36 = f32[32,48,192]{2,1,0:T(8,128)} all-to-all(f32[32,48,192]{2,1,0:T(8,128)} %convolution_bitcast_fusion), channel_id=1, replica_groups=mesh['rep'=2,'tp_0'=16,'tp_1'=2,'sub'=4] {'tp_0','tp_1'}, dimensions={0} | all-to-all | bytes 2359296 | tf_op jit(solution)/shard_map/all_to_all | solution.py:77
  476.8 9.4 %all_to_all.37 = bf16[4,12,192]{2,1,0:T(8,128)(2,1)S(1)} all-to-all(bf16[4,12,192]{2,1,0:T(8,128)(2,1)S(1)} %reshape.1223), channel_id=1, replica_groups=mesh['rep'=2,'tp_0'=16,'tp_1'=2,'sub'=4] {'sub'}, dimensions={0} | all-to-all | bytes 36864 | tf_op jit(solution)/shard_map/all_to_all | solution.py:185
  (142 shorter events, 86.0 us)
Async XLA Ops:
  6.5 379.3 %copy-start = (bf16[1,6144,256]{2,1,0:T(8,128)(2,1)S(1)}, bf16[1,6144,256]{2,1,0:T(8,128)(2,1)}, u32[]{:S(2)}) copy-start(bf16[1,6144,256]{2,1,0:T(8,128)(2,1)} %param.26) | copy-start | bytes 9437188
  8.1 66.0 %all-to-all-start = ((bf16[32,16,192]{2,1,0:T(8,128)(2,1)}), bf16[32,16,192]{2,1,0:T(8,128)(2,1)S(1)}, u32[]{:S(2)}, u32[]{:S(2)}) async-start(bf16[32,16,192]{2,1,0:T(8,128)(2,1)} %stack.2), calls=%async_computation | async-start | bytes 524288 | tf_op jit(solution)/shard_map/all_to_all | solution.py:111
  32.9 247.5 %all-gather.6.cloned.1.call-start = ((), (), s32[]{:S(2)}) async-start(), calls=%async_computation.7 | async-start | bytes 6684672 | tf_op jit(solution)/shard_map/all_gather | solution.py:27
  76.5 2.0 copy-start.6
  78.5 0.8 copy-start.1
  81.9 7.4 %copy-start.2 = (bf16[16,1024]{0,1:T(8,128)(2,1)S(1)}, bf16[16,1024]{0,1:T(8,128)(2,1)}, u32[]{:S(2)}) copy-start(bf16[16,1024]{0,1:T(8,128)(2,1)} %get-tuple-element.57) | copy-start | bytes 98308
  84.6 192.3 %all-to-all-start.1 = ((bf16[4,1536,192]{1,2,0:T(8,128)(2,1)}), bf16[4,1536,192]{1,2,0:T(8,128)(2,1)}, u32[]{:S(2)}, u32[]{:S(2)}) async-start(bf16[4,1536,192]{1,2,0:T(8,128)(2,1)} %broadcast_in_dim.20), calls=%async_computation.1 | async-start | bytes 4718592 | tf_op jit(solution)/shard_map/all_to_all | solution.py:42
  154.5 66.9 %copy-start.3 = (f32[16,8,6]{0,1,2:T(8,128)S(1)}, f32[16,8,6]{0,1,2:T(8,128)}, u32[]{:S(2)}) copy-start(f32[16,8,6]{0,1,2:T(8,128)} %copy.411) | copy-start | bytes 9220
  154.5 66.9 %copy-start.4 = (f32[16,8,6]{0,1,2:T(8,128)S(1)}, f32[16,8,6]{0,1,2:T(8,128)}, u32[]{:S(2)}) copy-start(f32[16,8,6]{0,1,2:T(8,128)} %copy.409) | copy-start | bytes 9220
  280.3 9.8 %copy-start.5 = (f32[16,8,128]{2,1,0:T(8,128)S(1)}, f32[16,8,128]{2,1,0:T(8,128)}, u32[]{:S(2)}) copy-start(f32[16,8,128]{2,1,0:T(8,128)} %copy.374) | copy-start | bytes 196612
  280.3 9.8 %copy-start.7 = (f32[16,8,6]{1,2,0:T(8,128)S(1)}, f32[16,8,6]{1,2,0:T(8,128)}, u32[]{:S(2)}) copy-start(f32[16,8,6]{1,2,0:T(8,128)} %copy.371) | copy-start | bytes 9220
  280.3 9.8 %copy-start.8 = (f32[16,8,6]{1,2,0:T(8,128)S(1)}, f32[16,8,6]{1,2,0:T(8,128)}, u32[]{:S(2)}) copy-start(f32[16,8,6]{1,2,0:T(8,128)} %copy.372) | copy-start | bytes 9220
  280.4 9.8 %copy-start.9 = (f32[16,8,6]{1,2,0:T(8,128)S(1)}, f32[16,8,6]{1,2,0:T(8,128)}, u32[]{:S(2)}) copy-start(f32[16,8,6]{1,2,0:T(8,128)} %copy.373) | copy-start | bytes 9220
  280.4 9.8 %copy-start.10 = (f32[16,8,6]{1,2,0:T(8,128)S(1)}, f32[16,8,6]{1,2,0:T(8,128)}, u32[]{:S(2)}) copy-start(f32[16,8,6]{1,2,0:T(8,128)} %copy.393) | copy-start | bytes 9220
  287.7 3.9 copy-start.11
  287.7 17.4 %copy-start.14 = (bf16[192]{0:T(256)(128)(2,1)S(1)}, bf16[192]{0:T(256)(128)(2,1)}, u32[]{:S(2)}) copy-start(bf16[192]{0:T(256)(128)(2,1)} %param.22) | copy-start | bytes 1156
  287.7 29.2 %copy-start.13 = (bf16[192,4]{0,1:T(4,128)(2,1)S(1)}, bf16[192,4]{0,1:T(4,128)(2,1)}, u32[]{:S(2)}) copy-start(bf16[192,4]{0,1:T(4,128)(2,1)} %param.23) | copy-start | bytes 4612
  287.8 34.8 %copy-start.12 = (s32[16,2]{0,1:T(2,128)S(1)}, s32[16,2]{0,1:T(2,128)}, u32[]{:S(2)}) copy-start(s32[16,2]{0,1:T(2,128)} %param.24) | copy-start | bytes 388
  294.9 22.0 %all-to-all-start.2 = ((f32[32,1,16]{2,1,0:T(1,128)}), f32[32,1,16]{2,1,0:T(1,128)S(1)}, u32[]{:S(2)}, u32[]{:S(2)}) async-start(f32[32,1,16]{2,1,0:T(1,128)} %broadcast_in_dim.21), calls=%async_computation.2 | async-start | bytes 32768 | tf_op jit(solution)/shard_map/all_to_all | solution.py:42
  317.8 18.4 %all-to-all-start.3 = ((f32[32,16,4]{1,2,0:T(4,128)}), f32[32,16,4]{1,2,0:T(4,128)S(1)}, u32[]{:S(2)}, u32[]{:S(2)}) async-start(f32[32,16,4]{1,2,0:T(4,128)} %broadcast_in_dim.22), calls=%async_computation.3 | async-start | bytes 131072 | tf_op jit(solution)/shard_map/all_to_all | solution.py:42
  337.5 10.6 %all-to-all-start.4 = ((bf16[4,12,192]{2,1,0:T(8,128)(2,1)}), bf16[4,12,192]{2,1,0:T(8,128)(2,1)S(1)}, u32[]{:S(2)}, u32[]{:S(2)}) async-start(bf16[4,12,192]{2,1,0:T(8,128)(2,1)} %convolution_convert_fusion), calls=%async_computation.4 | async-start | bytes 65536 | tf_op jit(solution)/shard_map/all_to_all | solution.py:177
Sparse Core Ops, SparseCore 0:
  82.0 96.1 all-gather.5
